TPU v7x, 32 devices: a whole 2x2x4 slice. The times are simulated.
32 devices in a mesh: dp: 8 (over z, x), mp: 4 (over y, core).
Axes of the slice: x: 2, y: 2, z: 4, core: 2. Of those that a mesh axis runs over, the one named last changes fastest.
Arguments:
- z_star: bfloat16 [8, 257, 1280], P('dp', None, 'mp'), may hold values from -24 to 24
- cotangent: float32 [8, 257, 1280], P('dp', None, 'mp'), may hold values from -6 to 6
- w_qkv: bfloat16 [3, 1280, 1280], P(None, None, 'mp'), may hold values from -1 to 1
- w_out: bfloat16 [1280, 1280], P('mp'), may hold values from -0.15625 to 0.15625
Outputs:
- implicit: float32 [8, 257, 1280], P('dp', None, 'mp')
- grad_qkv: float32 [3, 1280, 1280], P(None, 'dp', 'mp')
- grad_out: float32 [1280, 1280], P('mp', 'dp')
All inputs are finite; a program needn't handle non-finite values.
Results may differ from a plain program's by a relative error of at most 0.0091.
Values may be sent and summed in bfloat16 or wider, within the bound.
A program may use at most 128 MiB of HBM per device.

v0:
```python
import math
import jax
import jax.numpy as jnp
from jax import lax
from jax.sharding import PartitionSpec as P

HD = 80
TERMS = 3
epsilon = 1e-06


def shards(z_star, cotangent, w_qkv, w_out):
    groups = lax.axis_size("mp")
    images, tokens, narrow = z_star.shape
    model_width = narrow * groups
    columns = w_qkv.shape[2]
    heads_here = columns // HD
    score_scale = HD ** (-0.5)
    position = lax.axis_index("mp")
    whole = lax.all_gather(z_star, "mp", axis=2, tiled=True)
    values = whole.astype(jnp.float32)
    centred = values - jnp.mean(values, axis=-1, keepdims=True)
    inv_std = lax.rsqrt(jnp.mean(centred * centred, axis=-1, keepdims=True) + epsilon)
    normal_f = centred * inv_std
    normal_b = normal_f.astype(jnp.bfloat16)
    flattened = normal_b.reshape(-1, model_width)

    def project(slot_index):
        result = jnp.dot(flattened, w_qkv[slot_index], preferred_element_type=jnp.float32)
        return result.astype(jnp.bfloat16).reshape(images, tokens, heads_here, HD)

    queries = project(0)
    key_vecs = project(1)
    val_vecs = project(2)
    scores = (
        jnp.einsum("bqhe,bkhe->bhqk", queries, key_vecs, preferred_element_type=jnp.float32)
        * score_scale
    )
    attn_probs = jax.nn.softmax(scores, axis=-1)
    probs_b = attn_probs.astype(jnp.bfloat16)
    attended = jnp.einsum("bhqk,bkhe->bqhe", probs_b, val_vecs, preferred_element_type=jnp.float32)
    attended = attended.astype(jnp.bfloat16).reshape(-1, columns)
    contract_first = (((0,), (0,)), ((), ()))
    contract_second = (((1,), (1,)), ((), ()))
    running = cotangent
    gathered = lax.all_gather(cotangent.astype(jnp.bfloat16), "mp", axis=2, tiled=True)
    cot_rows = gathered.reshape(-1, model_width)
    sum_q = None
    sum_o = None
    for term_index in range(TERMS):
        needs_input = term_index + 1 < TERMS
        att_grad = lax.dot_general(
            cot_rows, w_out, contract_second, preferred_element_type=jnp.float32
        )
        att_grad = att_grad.astype(jnp.bfloat16).reshape(images, tokens, heads_here, HD)
        grad_o = lax.dot_general(
            attended, cot_rows, contract_first, preferred_element_type=jnp.float32
        )
        prob_grad = jnp.einsum(
            "bqhe,bkhe->bhqk", att_grad, val_vecs, preferred_element_type=jnp.float32
        )
        rowdot = jnp.sum(attn_probs * prob_grad, axis=-1, keepdims=True)
        score_grad = (attn_probs * (prob_grad - rowdot) * score_scale).astype(jnp.bfloat16)
        q_grad = jnp.einsum(
            "bhqk,bkhe->bqhe", score_grad, key_vecs, preferred_element_type=jnp.float32
        ).astype(jnp.bfloat16)
        k_grad = jnp.einsum(
            "bhqk,bqhe->bkhe", score_grad, queries, preferred_element_type=jnp.float32
        ).astype(jnp.bfloat16)
        v_grad = jnp.einsum(
            "bhqk,bqhe->bkhe", probs_b, att_grad, preferred_element_type=jnp.float32
        ).astype(jnp.bfloat16)
        qkv_grads = [item.reshape(-1, columns) for item in (q_grad, k_grad, v_grad)]
        grad_q = jnp.stack(
            [
                lax.dot_general(flattened, item, contract_first, preferred_element_type=jnp.float32)
                for item in qkv_grads
            ]
        )
        in_part = None
        if needs_input:
            in_part = lax.dot_general(
                qkv_grads[0], w_qkv[0], contract_second, preferred_element_type=jnp.float32
            )
            in_part = in_part + lax.dot_general(
                qkv_grads[1], w_qkv[1], contract_second, preferred_element_type=jnp.float32
            )
            in_part = in_part + lax.dot_general(
                qkv_grads[2], w_qkv[2], contract_second, preferred_element_type=jnp.float32
            )
            in_part = in_part.reshape(images, tokens, model_width)
        grad_q, grad_o, in_part = (grad_q, grad_o, in_part)
        part_q, part_o = (grad_q, grad_o)
        if term_index == 0:
            sum_q, sum_o = (part_q, part_o)
        else:
            sum_q = sum_q + part_q
            sum_o = sum_o + part_o
        if needs_input:
            in_grad = lax.psum(in_part, "mp")
            row_mean = jnp.mean(in_grad, axis=-1, keepdims=True)
            row_dot = jnp.mean(in_grad * normal_f, axis=-1, keepdims=True)
            full_term = (in_grad - row_mean - normal_f * row_dot) * inv_std
            local_term, full_term = (
                lax.dynamic_slice_in_dim(full_term, position * narrow, narrow, 2),
                full_term,
            )
            running = running + local_term
            cot_rows = full_term.astype(jnp.bfloat16).reshape(-1, model_width)
    sum_q, sum_o = (
        lax.psum_scatter(sum_q, "dp", scatter_dimension=1, tiled=True),
        lax.psum_scatter(sum_o, "dp", scatter_dimension=1, tiled=True),
    )
    factor = 1.0 / math.sqrt(images * lax.axis_size("dp") * tokens)
    return (running, sum_q * factor, sum_o * factor)


def solution(mesh):
    return jax.shard_map(
        shards,
        mesh=mesh,
        in_specs=(P("dp", None, "mp"), P("dp", None, "mp"), P(None, None, "mp"), P("mp", None)),
        out_specs=(P("dp", None, "mp"), P(None, "dp", "mp"), P("mp", "dp")),
        check_vma=False,
    )
```

profile of v0, /device:TPU:0, one launch (start us, length us, event | category | flops | bytes accessed | tf_op | source)
XLA Modules:
  0.0 371.2 jit_solution(9127516188160858572)
XLA Ops:
  9.0 17.0 %all_gather.6 = bf16[1,257,1280]{1,0,2:T(2,128)(2,1)} all-gather(bf16[1,257,320]{1,0,2:T(2,128)(2,1)S(1)} %copy.102), channel_id=1, replica_groups=mesh['dp'=8,'mp'=4] {'mp'}, dimensions={2}, use_global_device_ids=true | all-gather | bytes 822400 | tf_op jit(solution)/shard_map/all_gather | solution.py:20
  26.0 3.8 %copy.103 = bf16[1,257,1280]{2,1,0:T(8,128)(2,1)S(1)} copy(bf16[1,257,1280]{1,0,2:T(2,128)(2,1)} %all_gather.6) | data formatting | bytes 1315840 | tf_op jit(solution)/shard_map/all_gather | solution.py:20
  30.3 2.0 convolution_convert_fusion.8
  36.2 15.6 %all_gather.7 = bf16[1,257,1280]{1,0,2:T(2,128)(2,1)} all-gather(bf16[1,257,320]{1,0,2:T(2,128)(2,1)S(1)} %copy.107), channel_id=1, replica_groups=mesh['dp'=8,'mp'=4] {'mp'}, dimensions={2}, use_global_device_ids=true | all-gather | bytes 822400 | tf_op jit(solution)/shard_map/all_gather | solution.py:46
  51.7 3.8 %copy.108 = bf16[1,257,1280]{2,1,0:T(8,128)(2,1)S(1)} copy(bf16[1,257,1280]{1,0,2:T(2,128)(2,1)} %all_gather.7) | data formatting | bytes 1315840 | tf_op jit(solution)/shard_map/all_gather | solution.py:46
  59.9 4.4 %fusion.65 = bf16[4,80,257]{2,1,0:T(8,128)(2,1)} fusion(bf16[257,4,80]{0,2,1:T(8,128)(2,1)S(1)} %bitcast.203, f32[4,257,257]{1,2,0:T(8,128)} %fusion.137, f32[4,257,257]{1,2,0:T(8,128)} %get-tuple-element.23, f32[4,257]{1,0:T(4,128)S(1)} %get-tuple-element.22), kind=kOutput, calls=%fused_computation.64 | convolution fusion | flops 44204256 | bytes 2446640 | tf_op jit(solution)/shard_map/bhqk,bqhe->bkhe/dot_general | solution.py:67
  64.3 4.5 %fusion.62 = bf16[4,80,257]{2,1,0:T(8,128)(2,1)} fusion(bf16[257,4,80]{0,2,1:T(8,128)(2,1)S(1)} %bitcast.208, f32[4,257,257]{1,2,0:T(8,128)} %fusion.137, f32[4,257,257]{1,2,0:T(8,128)} %get-tuple-element.23, f32[4,257]{1,0:T(4,128)S(1)} %get-tuple-element.22), kind=kOutput, calls=%fused_computation.63 | convolution fusion | flops 44204256 | bytes 2446640 | tf_op jit(solution)/shard_map/bhqk,bkhe->bqhe/dot_general | solution.py:64
  79.4 36.4 %all-reduce.3.cloned.1.call-done = f32[1,257,1280]{2,1,0:T(8,128)} async-done(((f32[1,257,1280]{2,1,0:T(8,128)}), f32[1,257,1280]{2,1,0:T(8,128)}) %all-reduce.3.cloned.1.call-update) | async-done | bytes 1315856 | tf_op jit(solution)/shard_map/psum | solution.py:100
  122.1 2.1 convolution_convert_fusion.2
  124.2 2.6 fusion.138
  126.8 4.6 %fusion.56 = bf16[4,80,257]{2,1,0:T(8,128)(2,1)} fusion(bf16[257,4,80]{0,2,1:T(8,128)(2,1)} %bitcast.206, f32[4,257,257]{1,2,0:T(8,128)} %fusion.138, f32[4,257,257]{1,2,0:T(8,128)} %get-tuple-element.23, f32[4,257]{1,0:T(4,128)S(1)} %get-tuple-element.22), kind=kOutput, calls=%fused_computation.61 | convolution fusion | flops 44204256 | bytes 2446640 | tf_op jit(solution)/shard_map/bhqk,bkhe->bqhe/dot_general | solution.py:64
  131.4 4.6 %fusion.59 = bf16[4,80,257]{2,1,0:T(8,128)(2,1)} fusion(bf16[257,4,80]{0,2,1:T(8,128)(2,1)} %bitcast.204, f32[4,257,257]{1,2,0:T(8,128)} %fusion.138, f32[4,257,257]{1,2,0:T(8,128)} %get-tuple-element.23, f32[4,257]{1,0:T(4,128)S(1)} %get-tuple-element.22), kind=kOutput, calls=%fused_computation.62 | convolution fusion | flops 44204256 | bytes 2446640 | tf_op jit(solution)/shard_map/bhqk,bqhe->bkhe/dot_general | solution.py:67
  139.7 2.8 fusion.6
  143.8 2.1 convolution_add_fusion.1
  145.9 36.5 %all-reduce.5.cloned.1.call-done = f32[1,257,1280]{2,1,0:T(8,128)} async-done(((f32[1,257,1280]{2,1,0:T(8,128)}), f32[1,257,1280]{2,1,0:T(8,128)}) %all-reduce.5.cloned.1.call-update) | async-done | bytes 1315856 | tf_op jit(solution)/shard_map/psum | solution.py:100
  186.3 2.1 convolution_add_fusion
  199.4 4.6 %fusion.50 = bf16[4,80,257]{2,1,0:T(8,128)(2,1)} fusion(bf16[257,4,80]{0,2,1:T(8,128)(2,1)S(1)} %bitcast.209, f32[4,257,257]{1,2,0:T(8,128)} %fusion.139, f32[4,257,257]{1,2,0:T(8,128)} %get-tuple-element.23, f32[4,257]{1,0:T(4,128)S(1)} %get-tuple-element.22), kind=kOutput, calls=%fused_computation.59 | convolution fusion | flops 44204256 | bytes 2446640 | tf_op jit(solution)/shard_map/bhqk,bkhe->bqhe/dot_general | solution.py:64
  204.0 2.9 convolution_bitcast_fusion.2
  206.9 3.9 %fusion.53 = bf16[4,80,257]{2,1,0:T(8,128)(2,1)S(1)} fusion(bf16[257,4,80]{0,2,1:T(8,128)(2,1)S(1)} %bitcast.205, f32[4,257,257]{1,2,0:T(8,128)} %fusion.139, f32[4,257,257]{1,2,0:T(8,128)} %get-tuple-element.23, f32[4,257]{1,0:T(4,128)S(1)} %get-tuple-element.22), kind=kOutput, calls=%fused_computation.60 | convolution fusion | flops 44204256 | bytes 2446640 | tf_op jit(solution)/shard_map/bhqk,bqhe->bkhe/dot_general | solution.py:67
  213.6 4.7 %fusion.4 = f32[3,1280,320]{1,2,0:T(8,128)} fusion(f32[1,1280,320]{1,2,0:T(8,128)S(1)} %copy-done.8, f32[1,1280,320]{1,2,0:T(8,128)S(1)} %copy-done.9, f32[1,1280,320]{1,2,0:T(8,128)S(1)} %copy-done.10, f32[1,1280,320]{1,2,0:T(8,128)} %convolution_bitcast_fusion.3, f32[1,1280,320]{1,2,0:T(8,128)} %convolution_bitcast_fusion.4, ...), kind=kLoop, calls=%fused_computation.5 | loop fusion | flops 9830400 | bytes 19660800 | tf_op jit(solution)/shard_map/add | solution.py:97
  218.3 9.1 %copy.136 = f32[3,1280,320]{2,0,1:T(4,128)} copy(f32[3,1280,320]{1,2,0:T(8,128)} %fusion.4) | data formatting | bytes 9830400
  227.4 10.4 %reshape.277 = f32[1280,960]{1,0:T(8,128)} reshape(f32[1280,3,320]{2,1,0:T(4,128)} %bitcast.174) | data formatting | bytes 9830400
  241.4 14.6 %reduce-scatter.5.cloned.1.call-done = f32[320,160]{0,1:T(8,128)} async-done(((f32[320,1280]{0,1:T(8,128)}), f32[320,160]{0,1:T(8,128)}) %reduce-scatter.5.cloned.1.call-update) | async-done | bytes 204816 | tf_op jit(solution)/shard_map/reduce_scatter | solution.py:112
  257.6 103.8 %reduce-scatter.7.cloned.1.call-done = f32[160,960]{1,0:T(8,128)} async-done(((f32[1280,960]{1,0:T(8,128)}), f32[160,960]{1,0:T(8,128)}) %reduce-scatter.7.cloned.1.call-update) | async-done | bytes 614416
  (119 shorter events, 58.3 us)
Async XLA Ops:
  7.2 48.4 %copy-start = (bf16[320,1280]{1,0:T(8,128)(2,1)S(1)}, bf16[320,1280]{1,0:T(8,128)(2,1)}, u32[]{:S(2)}) copy-start(bf16[320,1280]{1,0:T(8,128)(2,1)} %param.7) | copy-start | bytes 2457604
  7.2 108.6 %all-reduce.3.cloned.1.call-start = ((), (), s32[]{:S(2)}) async-start(), calls=%async_computation.2 | async-start | bytes 2703360 | tf_op jit(solution)/shard_map/psum | solution.py:100
  30.0 2.3 copy-start.5
  35.1 24.8 %copy-start.25 = (bf16[257,320]{0,1:T(8,128)(2,1)}, bf16[257,320]{0,1:T(8,128)(2,1)S(1)}, u32[]{:S(2)}) copy-start(bf16[257,320]{0,1:T(8,128)(2,1)S(1)} %copy.105) | copy-start | bytes 493444
  56.1 1.9 copy-start.27
  56.3 3.6 copy-start.15
  68.8 3.3 copy-start.6
  68.8 3.3 copy-start.18
  70.6 2.0 copy-start.23
  74.9 107.6 %all-reduce.5.cloned.1.call-start = ((), (), s32[]{:S(2)}) async-start(), calls=%async_computation.3 | async-start | bytes 2703360 | tf_op jit(solution)/shard_map/psum | solution.py:100
  75.1 1.9 copy-start.24
  115.8 1.9 copy-start.11
  142.4 113.5 %reduce-scatter.5.cloned.1.call-start = ((), (), s32[]{:S(2)}) async-start(), calls=%async_computation.4 | async-start | bytes 2211840 | tf_op jit(solution)/shard_map/reduce_scatter | solution.py:112
  182.5 1.9 copy-start.12
  184.3 1.9 copy-start.7
  188.4 2.8 copy-start.14
  188.4 173.0 %reduce-scatter.7.cloned.1.call-start = ((), (), s32[]{:S(2)}) async-start(), calls=%async_computation.5 | async-start | bytes 5898240
  191.2 1.9 copy-start.22
  193.1 1.9 copy-start.20
  195.1 1.9 copy-start.4
  197.5 1.9 copy-start.28
  204.0 2.9 copy-start.26
  210.8 1.9 copy-start.10
  211.5 2.0 copy-start.9
  (9 other events, 11.6 us)
Sparse Core Ops, SparseCore 0:
  75.0 40.6 all-reduce.2
  142.6 39.8 all-reduce.4
  188.5 67.4 reduce-scatter.4
  259.4 101.9 reduce-scatter.6
where the time goes:
time: 372 us; the launch traced here: 371 us
  waiting for transfers between devices  191 us (51%)
  matrix products  74.3 us (20%)
  local copies, waits for them, and re-layouts  43.4 us (12%)
  blocking collectives  32.5 us (9%)
  other arithmetic  14.8 us (4%)
  between operations  14.2 us (4%)
    unnamed x5, waiting for transfers between devices  104 us
    psum x2, waiting for transfers between devices, shards(): in_grad = lax.psum(in_part, 'mp')  72.9 us
    unnamed x66, local copies, waits for them, and re-layouts  31.6 us
    all_gather x1, blocking collectives, shards(): whole = lax.all_gather(z_star, 'mp', axis=2, tiled=True)  17 us
    dot_general x9, matrix products, shards(): lax.dot_general(flattened, item, contract_first, preferred_element_type=j...  15.8 us
    all_gather x1, blocking collectives, shards(): lax.all_gather(cotangent.astype(jnp.bfloat16), 'mp', axis=2, tiled=True)  15.6 us
    reduce_scatter x1, waiting for transfers between devices, shards(): lax.psum_scatter(sum_o, 'dp', scatter_dimension=1, tiled=True)  14.6 us
    dot_general x3, matrix products, shards(): jnp.einsum('bhqk,bkhe->bqhe', score_grad, key_vecs, preferred_element_typ...  13.7 us
  transfers between devices with their start and end apart: 4, of which 4 were waited for; matrix products, arithmetic and copies ran while one was open for 16% of the time, Pallas kernels for 0%

commit v1 on v0

--- a/solution.py
+++ b/solution.py
@@ -43,7 +43,9 @@
     contract_first = (((0,), (0,)), ((), ()))
     contract_second = (((1,), (1,)), ((), ()))
     running = cotangent
-    gathered = lax.all_gather(cotangent.astype(jnp.bfloat16), "mp", axis=2, tiled=True)
+    part = cotangent.astype(jnp.bfloat16)
+    blocks = lax.all_gather(part, "mp")
+    gathered = jnp.concatenate(blocks, axis=2)
     cot_rows = gathered.reshape(-1, model_width)
     sum_q = None
     sum_o = None

time: 372 us -> 355 us (0.954)
  matrix products: 74.3 us -> 67.5 us
  blocking collectives: 32.5 us -> 25.8 us
  local copies, waits for them, and re-layouts: 43.4 us -> 38.3 us
    all_gather x1, blocking collectives: 15.6 us -> 8.86 us  [shards(): blocks = lax.all_gather(part, 'mp')]
    all_gather x1 -> x0, local copies, waits for them, and re-layouts: 3.79 us -> none  [shards(): lax.all_gather(cotangent.astype(jnp.bfloat16), 'mp', axis=2, tiled=True)]
    unnamed x66 -> x76, local copies, waits for them, and re-layouts: 31.6 us -> 32.1 us
where the time goes in v1:
time: 355 us; the launch traced here: 354 us
  waiting for transfers between devices  193 us (54%)
  matrix products  67.5 us (19%)
  local copies, waits for them, and re-layouts  38.3 us (11%)
  blocking collectives  25.8 us (7%)
  other arithmetic  14.8 us (4%)
  between operations  14.3 us (4%)
    unnamed x5, waiting for transfers between devices  104 us
    psum x2, waiting for transfers between devices, shards(): in_grad = lax.psum(in_part, 'mp')  73 us
    unnamed x76, local copies, waits for them, and re-layouts  32.1 us
    all_gather x1, blocking collectives, shards(): whole = lax.all_gather(z_star, 'mp', axis=2, tiled=True)  17 us
    reduce_scatter x1, waiting for transfers between devices, shards(): lax.psum_scatter(sum_o, 'dp', scatter_dimension=1, tiled=True)  16.3 us
    dot_general x9, matrix products, shards(): lax.dot_general(flattened, item, contract_first, preferred_element_type=j...  14.9 us
    dot_general x3, matrix products, shards(): jnp.einsum('bhqk,bqhe->bkhe', score_grad, queries, preferred_element_type...  11.5 us
    dot_general x3, matrix products, shards(): jnp.einsum('bhqk,bkhe->bqhe', score_grad, key_vecs, preferred_element_typ...  11.5 us
  transfers between devices with their start and end apart: 4, of which 4 were waited for; matrix products, arithmetic and copies ran while one was open for 16% of the time, Pallas kernels for 0%

profile of v1, /device:TPU:0, one launch (start us, length us, event | category | flops | bytes accessed | tf_op | source)
XLA Modules:
  0.0 354.4 jit_solution(11122001823822124913)
XLA Ops:
  9.0 17.0 %all_gather.9 = bf16[1,257,1280]{1,0,2:T(2,128)(2,1)} all-gather(bf16[1,257,320]{1,0,2:T(2,128)(2,1)S(1)} %copy.79), channel_id=1, replica_groups=mesh['dp'=8,'mp'=4] {'mp'}, dimensions={2}, use_global_device_ids=true | all-gather | bytes 822400 | tf_op jit(solution)/shard_map/all_gather | solution.py:20
  26.0 3.8 %copy.80 = bf16[1,257,1280]{2,1,0:T(8,128)(2,1)S(1)} copy(bf16[1,257,1280]{1,0,2:T(2,128)(2,1)} %all_gather.9) | data formatting | bytes 1315840 | tf_op jit(solution)/shard_map/all_gather | solution.py:20
  30.3 2.6 convolution_convert_fusion.8
  35.3 8.9 %all-gather = bf16[4,257,320]{2,1,0:T(8,128)(2,1)S(1)} all-gather(bf16[1,257,320]{2,1,0:T(8,128)(2,1)S(1)} %copy.116), channel_id=2, replica_groups=mesh['dp'=8,'mp'=4] {'mp'}, dimensions={0}, use_global_device_ids=true | all-gather | bytes 822400 | tf_op jit(solution)/shard_map/all_gather | solution.py:47
  50.9 3.8 %fusion.65 = bf16[4,80,257]{2,1,0:T(8,128)(2,1)S(1)} fusion(bf16[257,4,80]{0,2,1:T(8,128)(2,1)S(1)} %bitcast.204, f32[4,257,257]{1,2,0:T(8,128)} %fusion.134, f32[4,257,257]{1,2,0:T(8,128)} %get-tuple-element.20, f32[4,257]{1,0:T(4,128)S(1)} %get-tuple-element.19), kind=kOutput, calls=%fused_computation.64 | convolution fusion | flops 44204256 | bytes 2446640 | tf_op jit(solution)/shard_map/bhqk,bqhe->bkhe/dot_general | solution.py:69
  54.7 3.8 %fusion.62 = bf16[4,80,257]{2,1,0:T(8,128)(2,1)S(1)} fusion(bf16[257,4,80]{0,2,1:T(8,128)(2,1)S(1)} %bitcast.208, f32[4,257,257]{1,2,0:T(8,128)} %fusion.134, f32[4,257,257]{1,2,0:T(8,128)} %get-tuple-element.20, f32[4,257]{1,0:T(4,128)S(1)} %get-tuple-element.19), kind=kOutput, calls=%fused_computation.63 | convolution fusion | flops 44204256 | bytes 2446640 | tf_op jit(solution)/shard_map/bhqk,bkhe->bqhe/dot_general | solution.py:66
  65.7 1.9 convolution_bitcast_fusion.7
  68.1 36.4 %all-reduce.3.cloned.1.call-done = f32[1,257,1280]{2,1,0:T(8,128)} async-done(((f32[1,257,1280]{2,1,0:T(8,128)}), f32[1,257,1280]{2,1,0:T(8,128)}) %all-reduce.3.cloned.1.call-update) | async-done | bytes 1315856 | tf_op jit(solution)/shard_map/psum | solution.py:102
  111.4 3.8 %fusion.56 = bf16[4,80,257]{2,1,0:T(8,128)(2,1)S(1)} fusion(bf16[257,4,80]{0,2,1:T(8,128)(2,1)S(1)} %bitcast.209, f32[4,257,257]{1,2,0:T(8,128)} %fusion.135, f32[4,257,257]{1,2,0:T(8,128)} %get-tuple-element.20, f32[4,257]{1,0:T(4,128)S(1)} %get-tuple-element.19), kind=kOutput, calls=%fused_computation.61 | convolution fusion | flops 44204256 | bytes 2446640 | tf_op jit(solution)/shard_map/bhqk,bkhe->bqhe/dot_general | solution.py:66
  115.3 3.8 %fusion.59 = bf16[4,80,257]{2,1,0:T(8,128)(2,1)S(1)} fusion(bf16[257,4,80]{0,2,1:T(8,128)(2,1)S(1)} %bitcast.205, f32[4,257,257]{1,2,0:T(8,128)} %fusion.135, f32[4,257,257]{1,2,0:T(8,128)} %get-tuple-element.20, f32[4,257]{1,0:T(4,128)S(1)} %get-tuple-element.19), kind=kOutput, calls=%fused_computation.62 | convolution fusion | flops 44204256 | bytes 2446640 | tf_op jit(solution)/shard_map/bhqk,bqhe->bkhe/dot_general | solution.py:69
  122.7 2.8 fusion.6
  126.9 2.1 convolution_add_fusion.1
  129.0 36.5 %all-reduce.5.cloned.1.call-done = f32[1,257,1280]{2,1,0:T(8,128)} async-done(((f32[1,257,1280]{2,1,0:T(8,128)}), f32[1,257,1280]{2,1,0:T(8,128)}) %all-reduce.5.cloned.1.call-update) | async-done | bytes 1315856 | tf_op jit(solution)/shard_map/psum | solution.py:102
  169.4 2.1 convolution_add_fusion
  174.3 1.9 convolution_bitcast_fusion.3
  176.2 1.9 convolution_bitcast_fusion.4
  178.2 1.9 convolution_bitcast_fusion.5
  182.5 3.9 %fusion.50 = bf16[4,80,257]{2,1,0:T(8,128)(2,1)S(1)} fusion(bf16[257,4,80]{0,2,1:T(8,128)(2,1)S(1)} %bitcast.210, f32[4,257,257]{1,2,0:T(8,128)} %fusion.136, f32[4,257,257]{1,2,0:T(8,128)} %get-tuple-element.20, f32[4,257]{1,0:T(4,128)S(1)} %get-tuple-element.19), kind=kOutput, calls=%fused_computation.59 | convolution fusion | flops 44204256 | bytes 2446640 | tf_op jit(solution)/shard_map/bhqk,bkhe->bqhe/dot_general | solution.py:66
  188.3 3.9 %fusion.53 = bf16[4,80,257]{2,1,0:T(8,128)(2,1)S(1)} fusion(bf16[257,4,80]{0,2,1:T(8,128)(2,1)S(1)} %bitcast.206, f32[4,257,257]{1,2,0:T(8,128)} %fusion.136, f32[4,257,257]{1,2,0:T(8,128)} %get-tuple-element.20, f32[4,257]{1,0:T(4,128)S(1)} %get-tuple-element.19), kind=kOutput, calls=%fused_computation.60 | convolution fusion | flops 44204256 | bytes 2446640 | tf_op jit(solution)/shard_map/bhqk,bqhe->bkhe/dot_general | solution.py:69
  195.1 4.7 %fusion.4 = f32[3,1280,320]{1,2,0:T(8,128)} fusion(f32[1,1280,320]{1,2,0:T(8,128)S(1)} %copy-done.8, f32[1,1280,320]{1,2,0:T(8,128)S(1)} %copy-done.9, f32[1,1280,320]{1,2,0:T(8,128)S(1)} %copy-done.10, f32[1,1280,320]{1,2,0:T(8,128)} %convolution_bitcast_fusion.3, f32[1,1280,320]{1,2,0:T(8,128)} %convolution_bitcast_fusion.4, ...), kind=kLoop, calls=%fused_computation.5 | loop fusion | flops 9830400 | bytes 19660800 | tf_op jit(solution)/shard_map/add | solution.py:99
  199.8 9.1 %copy.112 = f32[3,1280,320]{2,0,1:T(4,128)} copy(f32[3,1280,320]{1,2,0:T(8,128)} %fusion.4) | data formatting | bytes 9830400
  208.9 10.4 %reshape.278 = f32[1280,960]{1,0:T(8,128)} reshape(f32[1280,3,320]{2,1,0:T(4,128)} %bitcast.174) | data formatting | bytes 9830400
  222.9 16.3 %reduce-scatter.5.cloned.1.call-done = f32[320,160]{0,1:T(8,128)} async-done(((f32[320,1280]{0,1:T(8,128)}), f32[320,160]{0,1:T(8,128)}) %reduce-scatter.5.cloned.1.call-update) | async-done | bytes 204816 | tf_op jit(solution)/shard_map/reduce_scatter | solution.py:114
  240.9 103.7 %reduce-scatter.7.cloned.1.call-done = f32[160,960]{1,0:T(8,128)} async-done(((f32[1280,960]{1,0:T(8,128)}), f32[160,960]{1,0:T(8,128)}) %reduce-scatter.7.cloned.1.call-update) | async-done | bytes 614416
  (129 shorter events, 52.9 us)
Async XLA Ops:
  7.2 38.4 %copy-start = (bf16[320,1280]{1,0:T(8,128)(2,1)S(1)}, bf16[320,1280]{1,0:T(8,128)(2,1)}, u32[]{:S(2)}) copy-start(bf16[320,1280]{1,0:T(8,128)(2,1)} %param.7) | copy-start | bytes 2457604
  7.2 97.3 %all-reduce.3.cloned.1.call-start = ((), (), s32[]{:S(2)}) async-start(), calls=%async_computation.2 | async-start | bytes 2703360 | tf_op jit(solution)/shard_map/psum | solution.py:102
  30.0 3.0 copy-start.5
  46.9 4.0 %copy-start.25 = (bf16[257,320]{0,1:T(8,128)(2,1)}, bf16[257,320]{0,1:T(8,128)(2,1)S(1)}, u32[]{:S(2)}) copy-start(bf16[257,320]{0,1:T(8,128)(2,1)S(1)} %copy.82) | copy-start | bytes 493444
  47.3 3.6 %copy-start.28 = (bf16[257,320]{0,1:T(8,128)(2,1)}, bf16[257,320]{0,1:T(8,128)(2,1)S(1)}, u32[]{:S(2)}) copy-start(bf16[257,320]{0,1:T(8,128)(2,1)S(1)} %copy.81) | copy-start | bytes 493444
  50.9 3.8 %copy-start.29 = (bf16[257,320]{0,1:T(8,128)(2,1)S(1)}, bf16[257,320]{0,1:T(8,128)(2,1)}, u32[]{:S(2)}) copy-start(bf16[257,320]{0,1:T(8,128)(2,1)} %copy-done.28) | copy-start | bytes 493444
  58.5 2.3 copy-start.19
  58.5 2.3 copy-start.6
  63.6 101.9 %all-reduce.5.cloned.1.call-start = ((), (), s32[]{:S(2)}) async-start(), calls=%async_computation.3 | async-start | bytes 2703360 | tf_op jit(solution)/shard_map/psum | solution.py:102
  108.6 2.8 copy-start.30
  111.4 3.8 %copy-start.26 = (bf16[257,320]{0,1:T(8,128)(2,1)S(1)}, bf16[257,320]{0,1:T(8,128)(2,1)}, u32[]{:S(2)}) copy-start(bf16[257,320]{0,1:T(8,128)(2,1)} %copy-done.25) | copy-start | bytes 493444
  115.2 3.9 %copy-start.21 = (bf16[4,80,257]{2,1,0:T(8,128)(2,1)}, bf16[4,80,257]{2,1,0:T(8,128)(2,1)S(1)}, u32[]{:S(2)}) copy-start(bf16[4,80,257]{2,1,0:T(8,128)(2,1)S(1)} %fusion.56) | copy-start | bytes 493444
  119.1 3.5 copy-start.23
  122.6 2.9 copy-start.14
  125.5 113.7 %reduce-scatter.5.cloned.1.call-start = ((), (), s32[]{:S(2)}) async-start(), calls=%async_computation.4 | async-start | bytes 2211840 | tf_op jit(solution)/shard_map/reduce_scatter | solution.py:114
  167.4 1.9 copy-start.7
  171.5 2.8 copy-start.16
  171.5 173.1 %reduce-scatter.7.cloned.1.call-start = ((), (), s32[]{:S(2)}) async-start(), calls=%async_computation.5 | async-start | bytes 5898240
  174.3 1.9 copy-start.24
  176.2 2.0 copy-start.22
  178.2 1.9 copy-start.4
  186.4 1.9 copy-start.27
  192.2 1.9 copy-start.10
  193.0 2.1 copy-start.9
  (14 other events, 19.7 us)
Sparse Core Ops, SparseCore 0:
  63.7 40.7 all-reduce.2
  125.6 39.8 all-reduce.4
  171.6 67.5 reduce-scatter.4
  242.7 101.8 reduce-scatter.6
